TPU v7x, 32 devices: a whole 2x2x4 slice. The times are simulated.
32 devices in a mesh: scen: 16 (over z, y, x), fac: 2 (over core).
Axes of the slice: x: 2, y: 2, z: 4, core: 2. Of those that a mesh axis runs over, the one named last changes fastest.
Arguments:
- scenario_pnl: float32 [16384, 2048], P('scen', 'fac'), may hold values from -300 to 300
Outputs:
- covariance: float32 [2048, 2048], P('scen', 'fac')
- factor_means: float32 [2048], P('fac')
All inputs are finite; a program needn't handle non-finite values.
Results may differ from a plain program's by a relative error of at most 0.0003.
Values sent between devices are 32-bit elements; how exact they have to be, the bound alone decides.
A program may use at most 64 MiB of HBM per device.

v0:
```python
import jax
import jax.numpy as jnp
from jax import lax
from jax.sharding import PartitionSpec as P


def block_gram(left, right):
    return lax.dot_general(
        left,
        right,
        (((0,), (0,)), ((), ())),
        precision=lax.Precision.HIGHEST,
        preferred_element_type=jnp.float32,
    )


def on_device(scenario_pnl):
    rows_here = scenario_pnl.shape[0]
    total_rows = rows_here * lax.axis_size("scen")
    local_sums = jnp.sum(scenario_pnl, axis=0)
    total_sums = lax.psum(local_sums, "scen")
    factor_means = total_sums / total_rows
    local_means = local_sums / rows_here
    data = scenario_pnl - local_means[None, :]
    partial_value = block_gram(lax.all_gather(data, "fac", axis=1, tiled=True), data)
    owned = lax.psum_scatter(partial_value, "scen", scatter_dimension=0, tiled=True)
    gathered = lax.all_gather(local_means, ("scen", "fac"), axis=0, tiled=True)
    spread_rows = gathered.reshape(lax.axis_size("scen"), -1)
    deviations = spread_rows - jnp.mean(spread_rows, axis=0, keepdims=True)
    owned_rows = owned.shape[0]
    column_width = owned.shape[1]
    row_part = lax.dynamic_slice_in_dim(
        deviations, lax.axis_index("scen") * owned_rows, owned_rows, 1
    )
    column_part = lax.dynamic_slice_in_dim(
        deviations, lax.axis_index("fac") * column_width, column_width, 1
    )
    owned = owned + rows_here * block_gram(row_part, column_part)
    covariance = owned / (total_rows - 1)
    return (covariance, factor_means)


def solution(mesh):
    return jax.shard_map(
        on_device,
        mesh=mesh,
        in_specs=(P("scen", "fac"),),
        out_specs=(P("scen", "fac"), P("fac")),
        check_vma=False,
    )
```

profile of v0, /device:TPU:1, one launch (start us, length us, event | category | flops | bytes accessed | tf_op | source)
XLA Modules:
  0.0 258.7 jit_solution(8484834909079317483)
XLA Ops:
  7.2 0.0 all-gather.2.cloned.1.call-start
  7.2 2.5 reduce_sum.18
  9.7 5.0 %broadcast_subtract_fusion = f32[1024,1024]{1,0:T(8,128)} fusion(f32[1024,1024]{1,0:T(8,128)} %param.1, f32[1024]{0:T(1024)S(1)} %broadcast_multiply_fusion.2), kind=kLoop, calls=%fused_computation | loop fusion | flops 1048576 | bytes 8392704 | tf_op jit(solution)/shard_map/sub | solution.py:24
  14.7 0.0 all-gather.2.cloned.1.call-update
  14.7 0.0 reduce-scatter.2.cloned.1.call-start
  14.7 22.4 %all-gather.2.cloned.1.call-done = f32[1024,2048]{1,0:T(8,128)} async-done(((f32[1024,1024]{1,0:T(8,128)}), f32[1024,2048]{1,0:T(8,128)}) %all-gather.2.cloned.1.call-update) | async-done | bytes 8388624 | tf_op jit(solution)/shard_map/all_gather | solution.py:25
  37.1 31.2 %fusion.5 = f32[2048,1024]{1,0:T(8,128)} fusion(f32[1024,2048]{1,0:T(8,128)} %all-gather.2.cloned.1.call-done, f32[1024,1024]{1,0:T(8,128)} %broadcast_subtract_fusion), kind=kOutput, calls=%fused_computation.11 | convolution fusion | flops 25769803776 | bytes 20971520 | tf_op jit(solution)/shard_map/dot_general | solution.py:8
  68.4 0.0 reduce-scatter.2.cloned.1.call-update
  68.4 46.7 %all_gather.7 = f32[32768]{0:T(1024)S(1)} all-gather(f32[1024]{0:T(1024)S(1)} %broadcast_multiply_fusion.2), channel_id=1, replica_groups=mesh['scen'=16,'fac'=2] {'scen','fac'}, dimensions={0}, use_global_device_ids=true | all-gather | bytes 135168 | tf_op jit(solution)/shard_map/all_gather | solution.py:27
  115.2 31.8 %psum.7 = f32[1024]{0:T(1024)S(1)} all-reduce(f32[1024]{0:T(1024)S(1)} %reduce_sum.18), channel_id=1, replica_groups=mesh['scen'=16,'fac'=2] {'scen'}, use_global_device_ids=true, to_apply=%region_3.0 | all-reduce | flops 1024 | bytes 8192 | tf_op jit(solution)/shard_map/psum | solution.py:21
  146.9 0.6 broadcast_multiply_fusion.1
  147.6 101.8 %reduce-scatter.2.cloned.1.call-done = f32[128,1024]{1,0:T(8,128)} async-done(((f32[2048,1024]{1,0:T(8,128)}), f32[128,1024]{1,0:T(8,128)}) %reduce-scatter.2.cloned.1.call-update) | async-done | bytes 524304 | tf_op jit(solution)/shard_map/reduce_scatter | solution.py:26
  249.3 2.5 fusion.1
  (5 shorter events, 0.1 us)
Async XLA Ops:
  7.2 30.0 %all-gather.2.cloned.1.call-start = ((), (), s32[]{:S(2)}) async-start(), calls=%async_computation.1 | async-start | bytes 12582912 | tf_op jit(solution)/shard_map/all_gather | solution.py:25
  14.7 234.7 %reduce-scatter.2.cloned.1.call-start = ((), (), s32[]{:S(2)}) async-start(), calls=%async_computation.2 | async-start | bytes 8912896 | tf_op jit(solution)/shard_map/reduce_scatter | solution.py:26
Sparse Core Ops, SparseCore 0:
  14.8 22.2 all-gather.1
  68.5 180.7 reduce-scatter.1
where the time goes:
time: 261 us; the launch traced here: 259 us
  waiting for transfers between devices  124 us (48%)
  blocking collectives  78.5 us (30%)
  matrix products  33.7 us (13%)
  between operations  14.1 us (5%)
  other arithmetic  8.09 us (3%)
    reduce_scatter x1, waiting for transfers between devices, on_device(): lax.psum_scatter(partial_value, 'scen', scatter_dimension=0, tiled=True)  102 us
    all_gather x1, blocking collectives, on_device(): gathered = lax.all_gather(local_means, ('scen', 'fac'), axis=0, tiled=True)  46.7 us
    dot_general x2, matrix products, block_gram(): lax.dot_general(left, right, (((0,), (0,)), ((), ())), precision=lax.Prec...  33.7 us
    psum x1, blocking collectives, on_device(): total_sums = lax.psum(local_sums, 'scen')  31.8 us
    all_gather x1, waiting for transfers between devices, on_device(): lax.all_gather(data, 'fac', axis=1, tiled=True)  22.4 us
  transfers between devices with their start and end apart: 2, of which 2 were waited for; matrix products, arithmetic and copies ran while one was open for 0% of the time, Pallas kernels for 0%

commit v1 on v0

--- a/solution.py
+++ b/solution.py
@@ -1,7 +1,15 @@
+import functools
+
 import jax
 import jax.numpy as jnp
 from jax import lax
+from jax.experimental import pallas as pl
+from jax.experimental.pallas import tpu as pltpu
 from jax.sharding import PartitionSpec as P
+
+MESH = pl.DeviceIdType.MESH
+LOADS = 4
+TILE = 64
 
 
 def block_gram(left, right):
@@ -40,9 +48,345 @@
     return (covariance, factor_means)
 
 
+def kernel(
+    n, x_hbm, cov_ref, mean_ref,
+    x_vm, other, hi_w, lo_w, hi_o, lo_o,
+    send1, keep1, recv1, send2, keep2, recv2, zsend, zrecv,
+    turned, landed, sums_own, sums_oth, dev_w, dev_o,
+    load_sem, pair_s, pair_r, s1_s, s1_r, s2_s, s2_r, z_s, z_r, t_s, t_r,
+    m_s, m_r, mo_s, mo_r,
+):
+    rows, width = x_hbm.shape
+    half = n // 2
+    block = width // half
+    near, far = half // 2 + 1, half // 2
+    depth = n // 4
+    zh = depth // 2
+    total_rows = rows * n
+
+    s = lax.axis_index("scen")
+    c = lax.axis_index("fac")
+    z, y, x = s // 4, (s // 2) % 2, s % 2
+    first = x * (1 - c) + y * c
+    second = y * (1 - c) + x * c
+    peer1 = s + (1 - 2 * x) * (1 - c) + (2 - 4 * y) * c
+    peer2 = s + (2 - 4 * y) * (1 - c) + (1 - 2 * x) * c
+
+    barrier = pltpu.get_barrier_semaphore()
+    me = s * 2 + c
+
+    def greet(d, carry):
+        p = (me + d) % (2 * n)
+        pl.semaphore_signal(barrier, inc=1, device_id=(p // 2, p % 2), device_id_type=MESH)
+        return carry
+
+    lax.fori_loop(1, 2 * n, greet, 0)
+
+    part = rows // LOADS
+    loads = []
+    for i in range(LOADS):
+        at = pl.ds(i * part, part)
+        load = pltpu.make_async_copy(x_hbm.at[at], x_vm.at[at], load_sem.at[i])
+        load.start()
+        loads.append(load)
+
+    def sums_of(ref, start, count, acc):
+        def add(i, acc):
+            at = pl.multiple_of(start + i * TILE, TILE)
+            return acc + jnp.sum(ref[pl.ds(at, TILE), :].reshape(TILE // 8, 8, width), axis=0)
+
+        return lax.fori_loop(0, count // TILE, add, acc)
+
+    acc = jnp.zeros((8, width), jnp.float32)
+    for i in range(LOADS):
+        loads[i].wait()
+        acc = sums_of(x_vm, i * part, part, acc)
+    local_sum = jnp.sum(acc, axis=0, keepdims=True)
+    sums_own[s] = local_sum
+    local_mean = local_sum / rows
+    mid = width // 2
+
+    def split_own(i, carry):
+        at = pl.ds(pl.multiple_of(i * TILE, TILE), TILE)
+        data = x_vm[at, :] - local_mean
+        hi = data.astype(jnp.bfloat16)
+        lo = (data - hi.astype(jnp.float32)).astype(jnp.bfloat16)
+        hi_w[at, :width] = hi
+        lo_w[at, :width] = lo
+        hi_w[at, width:] = hi[:, :mid]
+        lo_w[at, width:] = lo[:, :mid]
+        return carry
+
+    lax.fori_loop(0, rows // TILE, split_own, 0)
+
+    def split_other():
+        acc = sums_of(other, 0, rows, jnp.zeros((8, width), jnp.float32))
+        mean = jnp.sum(acc, axis=0, keepdims=True) / rows
+
+        def body(i, carry):
+            at = pl.ds(pl.multiple_of(i * TILE, TILE), TILE)
+            data = other[at, :] - mean
+            hi = data.astype(jnp.bfloat16)
+            hi_o[at, :] = hi
+            lo_o[at, :] = (data - hi.astype(jnp.float32)).astype(jnp.bfloat16)
+            return carry
+
+        lax.fori_loop(0, rows // TILE, body, 0)
+
+    def gram(left, right):
+        return lax.dot_general(
+            left, right, (((0,), (0,)), ((), ())), preferred_element_type=jnp.float32
+        )
+
+    def slot_of(k):
+        return c * zh + k if k < zh else (1 - c) * zh + k - zh
+
+    def width_of(k):
+        return (near if k < zh else far) * block
+
+    def compute(k, side, dst):
+        own = k < zh
+        wide = width_of(k)
+        hi_l, lo_l = (hi_w, lo_w) if own else (hi_o, lo_o)
+
+        def body(b, carry):
+            px = side * (1 - c) + b * c
+            py = b * (1 - c) + side * c
+            r = (slot_of(k) * 4 + py * 2 + px) % half
+            rows_at = pl.ds(pl.multiple_of(r * block, block), block)
+            start = r if own else r + c
+            cols_at = pl.ds(pl.multiple_of(start * block, block), wide)
+            lh, ll = hi_l[:, rows_at], lo_l[:, rows_at]
+            rh, rl = hi_w[:, cols_at], lo_w[:, cols_at]
+            dst[k, b, :, :wide] = gram(lh, rh) + (gram(lh, rl) + gram(ll, rh))
+            return carry
+
+        lax.fori_loop(0, 2, body, 0)
+
+    def remote(src, dst, send, recv, scen, fac):
+        return pltpu.make_async_remote_copy(
+            src_ref=src, dst_ref=dst, send_sem=send, recv_sem=recv,
+            device_id=(scen, fac), device_id_type=MESH,
+        )
+
+    def stage1(k):
+        w = width_of(k)
+        return remote(
+            send1.at[k, :, :, :w], recv1.at[k, :, :, :w], s1_s.at[k], s1_r.at[k], peer1, c
+        )
+
+    def stage2(k):
+        w = width_of(k)
+        return remote(send2.at[k, :, :w], recv2.at[k, :, :w], s2_s.at[k], s2_r.at[k], peer2, c)
+
+    def stage3(k):
+        w = width_of(k)
+        t = slot_of(k)
+        place = (z - t + depth - 1) % depth
+        return remote(
+            zsend.at[k, :, :w], zrecv.at[place, :, :w], z_s.at[k], z_r.at[place],
+            t * 4 + y * 2 + x, c,
+        )
+
+    def relay1(k):
+        w = width_of(k)
+        stage1(k).wait_recv()
+        send2[k, :, :w] = keep1[k, 1 - second, :, :w] + recv1[k, 1 - second, :, :w]
+        stage2(k).start()
+        keep2[k, :, :w] = keep1[k, second, :, :w] + recv1[k, second, :, :w]
+
+    def relay2(k):
+        w = width_of(k)
+        stage2(k).wait_recv()
+        zsend[k, :, :w] = keep2[k, :, :w] + recv2[k, :, :w]
+
+        @pl.when(slot_of(k) != z)
+        def _():
+            stage3(k).start()
+
+    compute(0, 1 - first, send1)
+    pl.semaphore_wait(barrier, 2 * n - 1)
+    stage1(0).start()
+    pair = remote(x_vm, other, pair_s, pair_r, s, 1 - c)
+    pair.start()
+
+    def mean_copy(d):
+        p = (s + d) % n
+        return remote(sums_own.at[s], sums_own.at[s], m_s.at[d], m_r.at[d], p, c)
+
+    for d in range(1, n):
+        mean_copy(d).start()
+
+    compute(0, first, keep1)
+    compute(1, 1 - first, send1)
+    stage1(1).start()
+    compute(1, first, keep1)
+
+    for d in range(1, n):
+        q = (s - d + n) % n
+        remote(sums_own.at[q], sums_own.at[q], m_s.at[d], m_r.at[d], q, c).wait_recv()
+    swap = remote(sums_own, sums_oth, mo_s, mo_r, s, 1 - c)
+    swap.start()
+
+    relay1(0)
+    pair.wait_recv()
+    split_other()
+    compute(2, 1 - first, send1)
+    stage1(2).start()
+    relay1(1)
+    compute(2, first, keep1)
+    relay2(0)
+    compute(3, 1 - first, send1)
+    stage1(3).start()
+    compute(3, first, keep1)
+    relay2(1)
+
+    def deviations(ref):
+        sums = ref[...].reshape(n, width)
+        total = jnp.sum(sums, axis=0, keepdims=True)
+        return sums / rows - total / total_rows, total / total_rows
+
+    dev, means = deviations(sums_own)
+    mean_ref[...] = means
+    dev_w[:, :width] = dev
+    dev_w[:, width:] = dev[:, :mid]
+    swap.wait_recv()
+    dev_o[...] = deviations(sums_oth)[0]
+
+    relay1(2)
+    relay2(2)
+    relay1(3)
+    relay2(3)
+
+    r = s % half
+
+    def turn_copy(own, d):
+        if own:
+            return remote(
+                turned.at[d], landed.at[d], t_s.at[d], t_r.at[d], c * half + (r + d) % half, c
+            )
+        return remote(
+            turned.at[d], landed.at[d], t_s.at[d], t_r.at[d],
+            c * half + (r + c + d) % half, 1 - c,
+        )
+
+    def finish(own):
+        count = near if own else far
+        w = count * block
+        for k in (range(zh) if own else range(zh, 2 * zh)):
+            @pl.when(slot_of(k) == z)
+            def _():
+                for place in range(depth - 1):
+                    remote(
+                        zsend.at[k, :, :w], zrecv.at[place, :, :w], z_s.at[k], z_r.at[place],
+                        s, 1 - c,
+                    ).wait_recv()
+                left = (dev_w if own else dev_o)[:, pl.ds(pl.multiple_of(r * block, block), block)]
+                start = r if own else r + c
+                shift = block_gram(
+                    left, dev_w[:, pl.ds(pl.multiple_of(start * block, block), w)]
+                )
+                value = zsend[k, :, :w]
+                for place in range(depth - 1):
+                    value = value + zrecv[place, :, :w]
+                value = (value + rows * shift) / (total_rows - 1)
+                turns = range(1, near - 1) if own else range(far)
+                for d in turns:
+                    turned[d] = value[:, d * block:(d + 1) * block].T
+                    turn_copy(own, d).start()
+                for d in range(count):
+                    q = (start + d) % half
+                    cov_ref[:, pl.ds(pl.multiple_of(q * block, block), block)] = value[
+                        :, d * block:(d + 1) * block
+                    ]
+                for d in turns:
+                    turn_copy(own, d).wait_recv()
+                    q = (r - d + half) % half if own else (r - (1 - c) - d + 2 * half) % half
+                    cov_ref[:, pl.ds(pl.multiple_of(q * block, block), block)] = landed[d]
+                for d in turns:
+                    turn_copy(own, d).wait_send()
+
+    finish(True)
+    finish(False)
+
+    pair.wait_send()
+    swap.wait_send()
+    for d in range(1, n):
+        mean_copy(d).wait_send()
+    for k in range(2 * zh):
+        stage1(k).wait_send()
+        stage2(k).wait_send()
+
+        @pl.when(slot_of(k) != z)
+        def _():
+            stage3(k).wait_send()
+
+
+def by_kernel(n, scenario_pnl):
+    rows, width = scenario_pnl.shape
+    half = n // 2
+    block = width // half
+    near = half // 2 + 1
+    depth = n // 4
+    f32, bf16 = jnp.float32, jnp.bfloat16
+    dma = pltpu.SemaphoreType.DMA
+    covariance, factor_means = pl.pallas_call(
+        functools.partial(kernel, n),
+        out_shape=(
+            jax.ShapeDtypeStruct((block, width), f32),
+            jax.ShapeDtypeStruct((1, width), f32),
+        ),
+        in_specs=[pl.BlockSpec(memory_space=pl.ANY)],
+        out_specs=[pl.BlockSpec(memory_space=pltpu.VMEM)] * 2,
+        scratch_shapes=[
+            pltpu.VMEM((rows, width), f32),
+            pltpu.VMEM((rows, width), f32),
+            pltpu.VMEM((rows, width + width // 2), bf16),
+            pltpu.VMEM((rows, width + width // 2), bf16),
+            pltpu.VMEM((rows, width), bf16),
+            pltpu.VMEM((rows, width), bf16),
+            pltpu.VMEM((depth, 2, block, near * block), f32),
+            pltpu.VMEM((depth, 2, block, near * block), f32),
+            pltpu.VMEM((depth, 2, block, near * block), f32),
+            pltpu.VMEM((depth, block, near * block), f32),
+            pltpu.VMEM((depth, block, near * block), f32),
+            pltpu.VMEM((depth, block, near * block), f32),
+            pltpu.VMEM((depth, block, near * block), f32),
+            pltpu.VMEM((depth - 1, block, near * block), f32),
+            pltpu.VMEM((near - 1, block, block), f32),
+            pltpu.VMEM((near - 1, block, block), f32),
+            pltpu.VMEM((n, 1, width), f32),
+            pltpu.VMEM((n, 1, width), f32),
+            pltpu.VMEM((n, width + width // 2), f32),
+            pltpu.VMEM((n, width), f32),
+            dma((LOADS,)),
+            dma, dma,
+            dma((depth,)), dma((depth,)),
+            dma((depth,)), dma((depth,)),
+            dma((depth,)), dma((depth - 1,)),
+            dma((near - 1,)), dma((near - 1,)),
+            dma((n,)), dma((n,)),
+            dma, dma,
+        ],
+        compiler_params=pltpu.CompilerParams(
+            collective_id=0, has_side_effects=True, vmem_limit_bytes=60 * 1024 * 1024
+        ),
+    )(scenario_pnl)
+    return covariance, factor_means.reshape(width)
+
+
 def solution(mesh):
+    n, cores = mesh.shape["scen"], mesh.shape["fac"]
+
+    def body(scenario_pnl):
+        rows, width = scenario_pnl.shape
+        fits = cores == 2 and n % 16 == 0 and n // 4 == 4 and width % (n * 64) == 0
+        if fits and rows % (LOADS * TILE) == 0:
+            return by_kernel(n, scenario_pnl)
+        return on_device(scenario_pnl)
+
     return jax.shard_map(
-        on_device,
+        body,
         mesh=mesh,
         in_specs=(P("scen", "fac"),),
         out_specs=(P("scen", "fac"), P("fac")),

time: 261 us -> 77.8 us (0.30)
  waiting for transfers between devices: 124 us -> 0 us
  blocking collectives: 78.5 us -> 0 us
  Pallas kernels: 0 us -> 73.9 us
  matrix products: 33.7 us -> 0 us
  between operations: 14.1 us -> 0.64 us
  other arithmetic: 8.09 us -> 0 us
  local copies, waits for them, and re-layouts: 0.03 us -> 3.15 us
    reduce_scatter x1 -> x0, waiting for transfers between devices: 102 us -> none  [on_device(): lax.psum_scatter(partial_value, 'scen', scatter_dimension=0, tiled=True)]
    pallas_call x0 -> x1, Pallas kernels: none -> 73.9 us  [by_kernel(): pl.pallas_call(functools.partial(kernel, n), out_shape=(jax.ShapeDtypeStr...]
    all_gather x1 -> x0, blocking collectives: 46.7 us -> none  [on_device(): gathered = lax.all_gather(local_means, ('scen', 'fac'), axis=0, tiled=True)]
    dot_general x2 -> x0, matrix products: 33.7 us -> none  [block_gram(): lax.dot_general(left, right, (((0,), (0,)), ((), ())), precision=lax.Prec...]
    psum x1 -> x0, blocking collectives: 31.8 us -> none  [on_device(): total_sums = lax.psum(local_sums, 'scen')]
    all_gather x1 -> x0, waiting for transfers between devices: 22.4 us -> none  [on_device(): lax.all_gather(data, 'fac', axis=1, tiled=True)]
    sub x2 -> x0, other arithmetic: 4.99 us -> none  [the longest x1 4.97 us: on_device(): data = scenario_pnl - local_means[None, :]]
    unnamed x0 -> x2, local copies, waits for them, and re-layouts: none -> 3.15 us
  transfers between devices with their start and end apart: 2 -> 0, of which waited for: 2 -> 0; matrix products, arithmetic and copies ran while one was open for 0% -> 0% of each run, Pallas kernels for 0% -> 0%
where the time goes in v1:
time: 77.8 us; the launch traced here: 77.6 us
  Pallas kernels  73.9 us (95%)
  local copies, waits for them, and re-layouts  3.15 us (4%)
    pallas_call x1, Pallas kernels, by_kernel(): pl.pallas_call(functools.partial(kernel, n), out_shape=(jax.ShapeDtypeStr...  73.9 us
    unnamed x2, local copies, waits for them, and re-layouts  3.15 us

profile of v1, /device:TPU:1, one launch (start us, length us, event | category | flops | bytes accessed | tf_op | source)
XLA Modules:
  0.0 77.6 jit_solution(9223956421021509738)
XLA Ops:
  0.6 73.9 %shard_map.30 = (f32[128,1024]{1,0:T(8,128)}, f32[1,1024]{1,0:T(1,128)}) custom-call(f32[1024,1024]{1,0:T(8,128)} %x_hbm.1), custom_call_target="tpu_custom_call" | custom-call | tf_op jit(solution)/shard_map/pallas_call | solution.py:333
  74.5 1.9 %copy.5 = f32[128,1024]{1,0:T(8,128)} copy(f32[128,1024]{1,0:T(8,128)} %get-tuple-element.8) | data formatting | bytes 1048576
  76.4 1.3 %copy.6 = f32[1024]{0:T(1024)} copy(f32[1024]{0:T(1024)} %bitcast.1) | data formatting | bytes 8192

commit v2 on v1

--- a/solution.py
+++ b/solution.py
@@ -51,7 +51,7 @@
 def kernel(
     n, x_hbm, cov_ref, mean_ref,
     x_vm, other, hi_w, lo_w, hi_o, lo_o,
-    send1, keep1, recv1, send2, keep2, recv2, zsend, zrecv,
+    send1, keep1, recv1, send2, recv2, zsend, zrecv,
     turned, landed, sums_own, sums_oth, dev_w, dev_o,
     load_sem, pair_s, pair_r, s1_s, s1_r, s2_s, s2_r, z_s, z_r, t_s, t_r,
     m_s, m_r, mo_s, mo_r,
@@ -75,13 +75,6 @@
     barrier = pltpu.get_barrier_semaphore()
     me = s * 2 + c
 
-    def greet(d, carry):
-        p = (me + d) % (2 * n)
-        pl.semaphore_signal(barrier, inc=1, device_id=(p // 2, p % 2), device_id_type=MESH)
-        return carry
-
-    lax.fori_loop(1, 2 * n, greet, 0)
-
     part = rows // LOADS
     loads = []
     for i in range(LOADS):
@@ -89,6 +82,13 @@
         load = pltpu.make_async_copy(x_hbm.at[at], x_vm.at[at], load_sem.at[i])
         load.start()
         loads.append(load)
+
+    def greet(d, carry):
+        p = (me + d) % (2 * n)
+        pl.semaphore_signal(barrier, inc=1, device_id=(p // 2, p % 2), device_id_type=MESH)
+        return carry
+
+    lax.fori_loop(1, 2 * n, greet, 0)
 
     def sums_of(ref, start, count, acc):
         def add(i, acc):
@@ -139,17 +139,19 @@
         )
 
     def slot_of(k):
-        return c * zh + k if k < zh else (1 - c) * zh + k - zh
+        turn = (k + z) % zh
+        return c * zh + turn if k < zh else (1 - c) * zh + turn
 
     def width_of(k):
         return (near if k < zh else far) * block
 
-    def compute(k, side, dst):
+    def compute(k, side, dst, send=False):
         own = k < zh
         wide = width_of(k)
         hi_l, lo_l = (hi_w, lo_w) if own else (hi_o, lo_o)
 
-        def body(b, carry):
+        def body(j, carry):
+            b = (1 - second) + j * (2 * second - 1)
             px = side * (1 - c) + b * c
             py = b * (1 - c) + side * c
             r = (slot_of(k) * 4 + py * 2 + px) % half
@@ -158,7 +160,9 @@
             cols_at = pl.ds(pl.multiple_of(start * block, block), wide)
             lh, ll = hi_l[:, rows_at], lo_l[:, rows_at]
             rh, rl = hi_w[:, cols_at], lo_w[:, cols_at]
-            dst[k, b, :, :wide] = gram(lh, rh) + (gram(lh, rl) + gram(ll, rh))
+            dst[k, j, :, :wide] = gram(lh, rh) + (gram(lh, rl) + gram(ll, rh))
+            if send:
+                stage1(k, j).start()
             return carry
 
         lax.fori_loop(0, 2, body, 0)
@@ -169,10 +173,10 @@
             device_id=(scen, fac), device_id_type=MESH,
         )
 
-    def stage1(k):
+    def stage1(k, j):
         w = width_of(k)
         return remote(
-            send1.at[k, :, :, :w], recv1.at[k, :, :, :w], s1_s.at[k], s1_r.at[k], peer1, c
+            send1.at[k, j, :, :w], recv1.at[k, j, :, :w], s1_s.at[k, j], s1_r.at[k, j], peer1, c
         )
 
     def stage2(k):
@@ -190,23 +194,22 @@
 
     def relay1(k):
         w = width_of(k)
-        stage1(k).wait_recv()
-        send2[k, :, :w] = keep1[k, 1 - second, :, :w] + recv1[k, 1 - second, :, :w]
+        stage1(k, 0).wait_recv()
+        send2[k, :, :w] = keep1[k, 0, :, :w] + recv1[k, 0, :, :w]
         stage2(k).start()
-        keep2[k, :, :w] = keep1[k, second, :, :w] + recv1[k, second, :, :w]
 
     def relay2(k):
         w = width_of(k)
+        stage1(k, 1).wait_recv()
         stage2(k).wait_recv()
-        zsend[k, :, :w] = keep2[k, :, :w] + recv2[k, :, :w]
+        zsend[k, :, :w] = keep1[k, 1, :, :w] + recv1[k, 1, :, :w] + recv2[k, :, :w]
 
         @pl.when(slot_of(k) != z)
         def _():
             stage3(k).start()
 
-    compute(0, 1 - first, send1)
     pl.semaphore_wait(barrier, 2 * n - 1)
-    stage1(0).start()
+    compute(0, 1 - first, send1, True)
     pair = remote(x_vm, other, pair_s, pair_r, s, 1 - c)
     pair.start()
 
@@ -218,8 +221,7 @@
         mean_copy(d).start()
 
     compute(0, first, keep1)
-    compute(1, 1 - first, send1)
-    stage1(1).start()
+    compute(1, 1 - first, send1, True)
     compute(1, first, keep1)
 
     for d in range(1, n):
@@ -231,15 +233,12 @@
     relay1(0)
     pair.wait_recv()
     split_other()
-    compute(2, 1 - first, send1)
-    stage1(2).start()
+    compute(2, 1 - first, send1, True)
     relay1(1)
     compute(2, first, keep1)
+    compute(3, 1 - first, send1, True)
     relay2(0)
-    compute(3, 1 - first, send1)
-    stage1(3).start()
     compute(3, first, keep1)
-    relay2(1)
 
     def deviations(ref):
         sums = ref[...].reshape(n, width)
@@ -254,8 +253,9 @@
     dev_o[...] = deviations(sums_oth)[0]
 
     relay1(2)
+    relay2(1)
+    relay1(3)
     relay2(2)
-    relay1(3)
     relay2(3)
 
     r = s % half
@@ -314,7 +314,8 @@
     for d in range(1, n):
         mean_copy(d).wait_send()
     for k in range(2 * zh):
-        stage1(k).wait_send()
+        stage1(k, 0).wait_send()
+        stage1(k, 1).wait_send()
         stage2(k).wait_send()
 
         @pl.when(slot_of(k) != z)
@@ -351,7 +352,6 @@
             pltpu.VMEM((depth, block, near * block), f32),
             pltpu.VMEM((depth, block, near * block), f32),
             pltpu.VMEM((depth, block, near * block), f32),
-            pltpu.VMEM((depth, block, near * block), f32),
             pltpu.VMEM((depth - 1, block, near * block), f32),
             pltpu.VMEM((near - 1, block, block), f32),
             pltpu.VMEM((near - 1, block, block), f32),
@@ -361,7 +361,7 @@
             pltpu.VMEM((n, width), f32),
             dma((LOADS,)),
             dma, dma,
-            dma((depth,)), dma((depth,)),
+            dma((depth, 2)), dma((depth, 2)),
             dma((depth,)), dma((depth,)),
             dma((depth,)), dma((depth - 1,)),
             dma((near - 1,)), dma((near - 1,)),

time: 77.8 us -> 71.1 us (0.914)
  Pallas kernels: 73.9 us -> 67.1 us
    pallas_call x1, Pallas kernels: 73.9 us -> 67.1 us  [by_kernel(): pl.pallas_call(functools.partial(kernel, n), out_shape=(jax.ShapeDtypeStr...]
where the time goes in v2:
time: 71.1 us; the launch traced here: 70.9 us
  Pallas kernels  67.1 us (94%)
  local copies, waits for them, and re-layouts  3.15 us (4%)
    pallas_call x1, Pallas kernels, by_kernel(): pl.pallas_call(functools.partial(kernel, n), out_shape=(jax.ShapeDtypeStr...  67.1 us
    unnamed x2, local copies, waits for them, and re-layouts  3.15 us

profile of v2, /device:TPU:1, one launch (start us, length us, event | category | flops | bytes accessed | tf_op | source)
XLA Modules:
  0.0 70.9 jit_solution(17153724880274529427)
XLA Ops:
  0.6 67.1 %shard_map.30 = (f32[128,1024]{1,0:T(8,128)}, f32[1,1024]{1,0:T(1,128)}) custom-call(f32[1024,1024]{1,0:T(8,128)} %x_hbm.1), custom_call_target="tpu_custom_call" | custom-call | tf_op jit(solution)/shard_map/pallas_call | solution.py:334
  67.7 1.9 %copy.5 = f32[128,1024]{1,0:T(8,128)} copy(f32[128,1024]{1,0:T(8,128)} %get-tuple-element.8) | data formatting | bytes 1048576
  69.6 1.3 %copy.6 = f32[1024]{0:T(1024)} copy(f32[1024]{0:T(1024)} %bitcast.1) | data formatting | bytes 8192
